TPU v7x, 256 devices: a whole 4x4x8 slice. The times are simulated.
256 devices in a mesh: bank: 64 (over z, y, core), zero: 4 (over x).
Axes of the slice: x: 4, y: 4, z: 8, core: 2. Of those that a mesh axis runs over, the one named last changes fastest.
Arguments:
- train_down: float32 [128, 768, 2048], P('bank', None, 'zero'), may hold values from -0.3125 to 0.3125
- other_down: float32 [128, 768, 2048], P('bank', None, 'zero'), may hold values from -0.21875 to 0.21875
- router_weight: float32 [2048, 128], P('zero', 'bank'), may hold values from -0.125 to 0.125
- router_gain: float32 [2048], P('zero'), may hold values from 0.25 to 1.75
Outputs:
- ready_down: bfloat16 [128, 768, 2048], P('bank')
- scale_down: float32 [128, 768], P('bank')
- serve_router: bfloat16 [2048, 128], replicated
- latest_down: float32 [128, 768, 2048], P('bank', None, 'zero')
All inputs are finite; a program needn't handle non-finite values. Where the computation divides by a largest or mean magnitude, that divisor is 1e-20 or more.
Results may differ from a plain program's by a relative error of at most 0.001.
Values may be sent and summed in bfloat16 or wider, within the bound.
A program may use at most 128 MiB of HBM per device.

v0:
```python
import jax
import jax.numpy as jnp
from jax import lax
from jax.sharding import Mesh
from jax.sharding import PartitionSpec as P

D_MODEL = 2048
BANK = ("bank_0", "bank_1", "bank_2")


def copy_for_each(x, axis):
    devices = lax.axis_size(axis)
    return lax.all_to_all(jnp.broadcast_to(x[None], (devices, *x.shape)), axis, 0, 0, tiled=True)


def of_everyone(x, axis):
    return copy_for_each(x, axis).sum(axis=0)


def in_order(blocks, dim):
    blocks = jnp.moveaxis(blocks, 0, dim)
    shape = blocks.shape
    return blocks.reshape(*shape[:dim], shape[dim] * shape[dim + 1], *shape[dim + 2 :])


def all_blocks(x, axes, turns):
    blocks = x
    for k in turns:
        blocks = lax.all_gather(blocks, axes[k])
    done = turns[::-1]
    back = [done.index(k) for k in range(len(axes))]
    blocks = blocks.transpose(*back, *range(len(axes), blocks.ndim))
    return blocks.reshape(-1, *x.shape)


def gather_axes(x, axes, turns, dim):
    return in_order(all_blocks(x, axes, turns), dim)


def shards(train_down, other_down, router_weight, router_gain):
    latest_down = 0.5 * other_down + 0.5 * train_down
    total_down = of_everyone(jnp.sum(jnp.abs(latest_down), axis=2), "zero")
    scale_down = total_down / D_MODEL
    narrow_down = (latest_down / jnp.expand_dims(scale_down, 2)).astype(jnp.bfloat16)
    ready_down = lax.all_gather(narrow_down, "zero", axis=2, tiled=True)
    part_router = (router_weight * router_gain[:, None]).astype(jnp.bfloat16)
    row_router = lax.all_gather(part_router, "zero", axis=0, tiled=True)
    serve_router = gather_axes(row_router, BANK, (1, 0, 2), 1)
    return (ready_down, scale_down, serve_router, latest_down)


def solution(mesh):
    split = Mesh(
        mesh.devices.reshape(8, 4, 2, mesh.shape["zero"]), ("bank_0", "bank_1", "bank_2", "zero")
    )
    placed = (P(BANK, None, "zero"), P(BANK, None, "zero"), P("zero", BANK), P("zero"))
    return jax.shard_map(
        shards,
        mesh=split,
        in_specs=placed,
        out_specs=(P(BANK, None, None), P(BANK, None), P(), P(BANK, None, "zero")),
        check_vma=False,
    )
```

profile of v0, /device:TPU:1, one launch (start us, length us, event | category | flops | bytes accessed | tf_op | source)
XLA Modules:
  0.0 105.1 jit_solution(9432049307572382526)
XLA Ops:
  7.2 0.0 all-gather.5.cloned.1.call-start
  7.2 3.3 %abs_reduce_fusion = (f32[2,768]{1,0:T(2,128)S(1)}, f32[2,768,512]{2,1,0:T(8,128)S(1)}) fusion(f32[2,768,512]{2,1,0:T(8,128)} %param.5, f32[2,768,512]{2,1,0:T(8,128)} %param.4), kind=kLoop, calls=%fused_computation.1 | loop fusion | flops 3144192 | bytes 9443328 | tf_op jit(solution)/shard_map/reduce_sum | solution.py:42
  10.6 0.0 copy-start
  10.6 8.9 %all_to_all.5 = f32[4,2,768]{2,1,0:T(2,128)S(1)} all-to-all(f32[4,2,768]{2,1,0:T(2,128)S(1)} %broadcast_in_dim.2), channel_id=1, replica_groups=mesh['bank_0'=8,'bank_1'=4,'bank_2'=2,'zero'=4] {'zero'}, dimensions={0} | all-to-all | bytes 49152 | tf_op jit(solution)/shard_map/all_to_all | solution.py:13
  19.5 0.0 copy-start.1
  19.5 0.0 copy-start.2
  19.5 0.0 copy-start.3
  19.5 1.4 %divide_convert_fusion = bf16[2,768,512]{2,1,0:T(8,128)(2,1)} fusion(f32[2,768,512]{2,1,0:T(8,128)S(1)} %get-tuple-element.33, f32[2,768]{1,0:T(2,128)S(1)} %broadcast_multiply_fusion), kind=kLoop, calls=%fused_computation | loop fusion | flops 1572864 | bytes 4724736 | tf_op jit(solution)/shard_map/convert_element_type | solution.py:44
  21.0 0.0 all-gather.5.cloned.1.call-update
  21.0 0.0 copy-done
  21.0 0.0 copy-done.1
  21.0 0.0 copy-done.2
  21.0 0.0 copy-done.3
  21.1 8.1 %all_gather.25 = bf16[2048,2]{0,1:T(2,128)(2,1)S(1)} all-gather(bf16[512,2]{0,1:T(2,128)(2,1)S(1)} %multiply_convert_fusion), channel_id=1, replica_groups=mesh['bank_0'=8,'bank_1'=4,'bank_2'=2,'zero'=4] {'zero'}, dimensions={0}, use_global_device_ids=true | all-gather | bytes 10240 | tf_op jit(solution)/shard_map/all_gather | solution.py:47
  29.2 9.5 %all-gather = bf16[8192,2]{0,1:T(2,128)(2,1)S(1)} all-gather(bf16[2048,2]{0,1:T(2,128)(2,1)S(1)} %all_gather.25), channel_id=2, replica_groups=mesh['bank_0'=8,'bank_1'=4,'bank_2'=2,'zero'=4] {'bank_1'}, dimensions={0}, use_global_device_ids=true | all-gather | bytes 40960 | tf_op jit(solution)/shard_map/all_gather | solution.py:29
  38.7 24.8 %all-gather.1 = bf16[32,2048,2]{1,2,0:T(2,128)(2,1)S(1)} all-gather(bf16[4,2048,2]{1,2,0:T(2,128)(2,1)S(1)} %bitcast.15), channel_id=3, replica_groups=mesh['bank_0'=8,'bank_1'=4,'bank_2'=2,'zero'=4] {'bank_0'}, dimensions={0}, use_global_device_ids=true | all-gather | bytes 294912 | tf_op jit(solution)/shard_map/all_gather | solution.py:29
  63.6 0.1 copy.22
  63.7 12.7 %all-gather.2 = bf16[16,4,2048,2]{2,1,3,0:T(4,128)(2,1)S(1)} all-gather(bf16[8,4,2048,2]{2,1,3,0:T(4,128)(2,1)S(1)} %copy.22), channel_id=4, replica_groups=mesh['bank_0'=8,'bank_1'=4,'bank_2'=2,'zero'=4] {'bank_2'}, dimensions={0}, use_global_device_ids=true | all-gather | bytes 786432 | tf_op jit(solution)/shard_map/all_gather | solution.py:29
  76.5 0.3 copy.28
  76.7 0.5 copy.24
  77.3 0.2 reshape.20
  77.5 1.0 copy.25
  78.5 13.2 %all-gather.5.cloned.1.call-done = bf16[2,768,2048]{2,1,0:T(8,128)(2,1)} async-done(((bf16[2,768,512]{2,1,0:T(8,128)(2,1)}), bf16[2,768,2048]{2,1,0:T(8,128)(2,1)}) %all-gather.5.cloned.1.call-update) | async-done | bytes 6291472 | tf_op jit(solution)/shard_map/all_gather | solution.py:45
  91.7 6.6 %copy.30 = bf16[2,768,2048]{2,1,0:T(8,128)(2,1)} copy(bf16[2,768,2048]{2,1,0:T(8,128)(2,1)} %all-gather.5.cloned.1.call-done) | data formatting | bytes 12582912
  (4 shorter events, 0.0 us)
Async XLA Ops:
  7.2 84.5 %all-gather.5.cloned.1.call-start = ((), (), s32[]{:S(2)}) async-start(), calls=%async_computation.1 | async-start | bytes 7864320 | tf_op jit(solution)/shard_map/all_gather | solution.py:45
  10.6 10.4 %copy-start = (f32[2,768,512]{2,1,0:T(8,128)}, f32[2,768,512]{2,1,0:T(8,128)S(1)}, u32[]{:S(2)}) copy-start(f32[2,768,512]{2,1,0:T(8,128)S(1)} %get-tuple-element.33) | copy-start | bytes 9437188
  19.5 1.5 %copy-start.1 = (f32[2,768]{1,0:T(2,128)}, f32[2,768]{1,0:T(2,128)S(1)}, u32[]{:S(2)}) copy-start(f32[2,768]{1,0:T(2,128)S(1)} %broadcast_multiply_fusion) | copy-start | bytes 18436
  19.5 1.5 %copy-start.2 = (f32[512,2]{0,1:T(2,128)S(1)}, f32[512,2]{0,1:T(2,128)}, u32[]{:S(2)}) copy-start(f32[512,2]{0,1:T(2,128)} %param.6) | copy-start | bytes 12292
  19.5 1.5 %copy-start.3 = (f32[512]{0:T(512)S(1)}, f32[512]{0:T(512)}, u32[]{:S(2)}) copy-start(f32[512]{0:T(512)} %param.7) | copy-start | bytes 6148
Sparse Core Ops, SparseCore 0:
  21.1 70.5 all-gather.4
where the time goes:
time: 105 us
  blocking collectives  64.1 us (61%)
  between operations  14.1 us (13%)
  waiting for transfers between devices  13.2 us (13%)
  local copies, waits for them, and re-layouts  8.81 us (8%)
  other arithmetic  4.81 us (5%)
    all_gather x3, blocking collectives, all_blocks(): blocks = lax.all_gather(blocks, axes[k])  47.1 us
    all_gather x1, waiting for transfers between devices, shards(): ready_down = lax.all_gather(narrow_down, 'zero', axis=2, tiled=True)  13.2 us
    all_to_all x1, blocking collectives, copy_for_each(): lax.all_to_all(jnp.broadcast_to(x[None], (devices, *x.shape)), axis, 0, 0...  8.89 us
    all_gather x1, blocking collectives, shards(): row_router = lax.all_gather(part_router, 'zero', axis=0, tiled=True)  8.14 us
    unnamed x10, local copies, waits for them, and re-layouts  7.64 us
    reduce_sum x1, other arithmetic, shards(): total_down = of_everyone(jnp.sum(jnp.abs(latest_down), axis=2), 'zero')  3.34 us
  transfers between devices with their start and end apart: 1, of which 1 were waited for; matrix products, arithmetic and copies ran while one was open for 2% of the time, Pallas kernels for 0%

commit v1 on v0

--- a/solution.py
+++ b/solution.py
@@ -42,7 +42,8 @@
     total_down = of_everyone(jnp.sum(jnp.abs(latest_down), axis=2), "zero")
     scale_down = total_down / D_MODEL
     narrow_down = (latest_down / jnp.expand_dims(scale_down, 2)).astype(jnp.bfloat16)
-    ready_down = lax.all_gather(narrow_down, "zero", axis=2, tiled=True)
+    terms = lax.all_gather(narrow_down, "zero", axis=0, tiled=False)
+    ready_down = jnp.concatenate(terms, axis=2)
     part_router = (router_weight * router_gain[:, None]).astype(jnp.bfloat16)
     row_router = lax.all_gather(part_router, "zero", axis=0, tiled=True)
     serve_router = gather_axes(row_router, BANK, (1, 0, 2), 1)

time: 105 us -> 105 us (level)
    unnamed x10 -> x9, local copies, waits for them, and re-layouts: 7.64 us -> 1.02 us
    reshape x0 -> x1, local copies, waits for them, and re-layouts: none -> 6.47 us  [shards(): ready_down = jnp.concatenate(terms, axis=2)]
where the time goes in v1:
time: 105 us
  blocking collectives  64.1 us (61%)
  between operations  14.1 us (13%)
  waiting for transfers between devices  13.2 us (13%)
  local copies, waits for them, and re-layouts  8.67 us (8%)
  other arithmetic  4.81 us (5%)
    all_gather x3, blocking collectives, all_blocks(): blocks = lax.all_gather(blocks, axes[k])  47.1 us
    all_gather x1, waiting for transfers between devices, shards(): terms = lax.all_gather(narrow_down, 'zero', axis=0, tiled=False)  13.2 us
    all_to_all x1, blocking collectives, copy_for_each(): lax.all_to_all(jnp.broadcast_to(x[None], (devices, *x.shape)), axis, 0, 0...  8.89 us
    all_gather x1, blocking collectives, shards(): row_router = lax.all_gather(part_router, 'zero', axis=0, tiled=True)  8.14 us
    reshape x1, local copies, waits for them, and re-layouts, shards(): ready_down = jnp.concatenate(terms, axis=2)  6.47 us
    reduce_sum x1, other arithmetic, shards(): total_down = of_everyone(jnp.sum(jnp.abs(latest_down), axis=2), 'zero')  3.34 us
  transfers between devices with their start and end apart: 1, of which 1 were waited for; matrix products, arithmetic and copies ran while one was open for 2% of the time, Pallas kernels for 0%

profile of v1, /device:TPU:1, one launch (start us, length us, event | category | flops | bytes accessed | tf_op | source)
XLA Modules:
  0.0 105.0 jit_solution(14287151314433224797)
XLA Ops:
  7.2 0.0 all-gather.6.cloned.1.call-start
  7.2 3.3 %abs_reduce_fusion = (f32[2,768]{1,0:T(2,128)S(1)}, f32[2,768,512]{2,1,0:T(8,128)S(1)}) fusion(f32[2,768,512]{2,1,0:T(8,128)} %param.5, f32[2,768,512]{2,1,0:T(8,128)} %param.4), kind=kLoop, calls=%fused_computation.1 | loop fusion | flops 3144192 | bytes 9443328 | tf_op jit(solution)/shard_map/reduce_sum | solution.py:42
  10.6 0.0 copy-start
  10.6 8.9 %all_to_all.5 = f32[4,2,768]{2,1,0:T(2,128)S(1)} all-to-all(f32[4,2,768]{2,1,0:T(2,128)S(1)} %broadcast_in_dim.2), channel_id=1, replica_groups=mesh['bank_0'=8,'bank_1'=4,'bank_2'=2,'zero'=4] {'zero'}, dimensions={0} | all-to-all | bytes 49152 | tf_op jit(solution)/shard_map/all_to_all | solution.py:13
  19.5 0.0 copy-start.1
  19.5 0.0 copy-start.2
  19.5 0.0 copy-start.3
  19.5 1.4 %divide_convert_fusion = bf16[2,768,512]{2,1,0:T(8,128)(2,1)} fusion(f32[2,768,512]{2,1,0:T(8,128)S(1)} %get-tuple-element.25, f32[2,768]{1,0:T(2,128)S(1)} %broadcast_multiply_fusion), kind=kLoop, calls=%fused_computation | loop fusion | flops 1572864 | bytes 4724736 | tf_op jit(solution)/shard_map/convert_element_type | solution.py:44
  21.0 0.0 all-gather.6.cloned.1.call-update
  21.0 0.0 copy-done
  21.0 0.0 copy-done.1
  21.0 0.0 copy-done.2
  21.0 0.0 copy-done.3
  21.1 8.1 %all_gather.29 = bf16[2048,2]{0,1:T(2,128)(2,1)S(1)} all-gather(bf16[512,2]{0,1:T(2,128)(2,1)S(1)} %multiply_convert_fusion), channel_id=1, replica_groups=mesh['bank_0'=8,'bank_1'=4,'bank_2'=2,'zero'=4] {'zero'}, dimensions={0}, use_global_device_ids=true | all-gather | bytes 10240 | tf_op jit(solution)/shard_map/all_gather | solution.py:48
  29.2 9.5 %all-gather.1 = bf16[8192,2]{0,1:T(2,128)(2,1)S(1)} all-gather(bf16[2048,2]{0,1:T(2,128)(2,1)S(1)} %all_gather.29), channel_id=3, replica_groups=mesh['bank_0'=8,'bank_1'=4,'bank_2'=2,'zero'=4] {'bank_1'}, dimensions={0}, use_global_device_ids=true | all-gather | bytes 40960 | tf_op jit(solution)/shard_map/all_gather | solution.py:29
  38.7 24.8 %all-gather.2 = bf16[32,2048,2]{1,2,0:T(2,128)(2,1)S(1)} all-gather(bf16[4,2048,2]{1,2,0:T(2,128)(2,1)S(1)} %bitcast.22), channel_id=4, replica_groups=mesh['bank_0'=8,'bank_1'=4,'bank_2'=2,'zero'=4] {'bank_0'}, dimensions={0}, use_global_device_ids=true | all-gather | bytes 294912 | tf_op jit(solution)/shard_map/all_gather | solution.py:29
  63.6 0.1 copy.28
  63.7 12.7 %all-gather.3 = bf16[16,4,2048,2]{2,1,3,0:T(4,128)(2,1)S(1)} all-gather(bf16[8,4,2048,2]{2,1,3,0:T(4,128)(2,1)S(1)} %copy.28), channel_id=5, replica_groups=mesh['bank_0'=8,'bank_1'=4,'bank_2'=2,'zero'=4] {'bank_2'}, dimensions={0}, use_global_device_ids=true | all-gather | bytes 786432 | tf_op jit(solution)/shard_map/all_gather | solution.py:29
  76.5 0.3 copy.35
  76.7 0.5 copy.30
  77.3 0.2 reshape.28
  77.5 1.0 copy.31
  78.5 13.2 %all-gather.6.cloned.1.call-done = bf16[8,768,512]{2,1,0:T(8,128)(2,1)} async-done(((bf16[2,768,512]{2,1,0:T(8,128)(2,1)}), bf16[8,768,512]{2,1,0:T(8,128)(2,1)}) %all-gather.6.cloned.1.call-update) | async-done | bytes 6291472 | tf_op jit(solution)/shard_map/all_gather | solution.py:45
  91.7 6.5 %copy.33 = bf16[4,2,96,8,512]{4,3,0,2,1:T(8,128)(2,1)} copy(bf16[4,2,96,8,512]{4,3,2,1,0:T(8,128)(2,1)} %bitcast.17) | data formatting | bytes 12582912 | tf_op jit(solution)/shard_map/reshape | solution.py:46
  (4 shorter events, 0.0 us)
Async XLA Ops:
  7.2 84.5 %all-gather.6.cloned.1.call-start = ((), (), s32[]{:S(2)}) async-start(), calls=%async_computation.1 | async-start | bytes 7864320 | tf_op jit(solution)/shard_map/all_gather | solution.py:45
  10.6 10.4 %copy-start = (f32[2,768,512]{2,1,0:T(8,128)}, f32[2,768,512]{2,1,0:T(8,128)S(1)}, u32[]{:S(2)}) copy-start(f32[2,768,512]{2,1,0:T(8,128)S(1)} %get-tuple-element.25) | copy-start | bytes 9437188
  19.5 1.5 %copy-start.1 = (f32[2,768]{1,0:T(2,128)}, f32[2,768]{1,0:T(2,128)S(1)}, u32[]{:S(2)}) copy-start(f32[2,768]{1,0:T(2,128)S(1)} %broadcast_multiply_fusion) | copy-start | bytes 18436
  19.5 1.5 %copy-start.2 = (f32[512,2]{0,1:T(2,128)S(1)}, f32[512,2]{0,1:T(2,128)}, u32[]{:S(2)}) copy-start(f32[512,2]{0,1:T(2,128)} %param.6) | copy-start | bytes 12292
  19.5 1.5 %copy-start.3 = (f32[512]{0:T(512)S(1)}, f32[512]{0:T(512)}, u32[]{:S(2)}) copy-start(f32[512]{0:T(512)} %param.7) | copy-start | bytes 6148
Sparse Core Ops, SparseCore 0:
  21.1 70.5 all-gather.5
